TPU v7x, 32 devices: a whole 2x2x4 slice. The times are simulated.
32 devices in a mesh: seq: 8 (over z, x), head: 4 (over y, core).
Axes of the slice: x: 2, y: 2, z: 4, core: 2. Of those that a mesh axis runs over, the one named last changes fastest.
Arguments:
- patches: bfloat16 [32768, 768], P('seq'), may hold values from -6 to 6
- slot_image: int32 [128], P('seq'), may hold values from -1 to 63, as said below
- slot_dest: int32 [128], P('seq'), may hold values from -1 to 63, as said below
- enc_gain: float32 [768], replicated, may hold values from 0.1 to 1.9
- w_qkv: bfloat16 [3, 768, 768], P(None, None, 'head'), may hold values from -1.2 to 1.2
- w_out: bfloat16 [768, 768], P('head'), may hold values from -0.21875 to 0.21875
- fast_gain: float32 [768], replicated, may hold values from 0.1 to 1.9
- w_fast: bfloat16 [3, 768, 768], P(None, None, 'head'), may hold values from -0.21875 to 0.21875
- w_rate: bfloat16 [768, 4], P(None, 'head'), may hold values from -0.21875 to 0.21875
- fast_gate_up: float32 [4, 2, 192, 384], P('head'), may hold values from -0.4375 to 0.4375
- fast_down: float32 [4, 384, 192], P('head'), may hold values from -0.3125 to 0.3125
Outputs:
- view_out: bfloat16 [16384, 768], P('seq', 'head')
Inputs may be any that keep to these rules, and one draw needn't show every extreme that they name: slot_dest gives for each slot the view-order block that its block becomes, or -1 for an empty slot; every view-order block is named by exactly one slot. Slots 2i and 2i + 1 of one seq index are both empty or name view blocks 2m and 2m + 1. The slots of one seq index name at most 2 blocks of any one view shard (blocks s * 8 to (s + 1) * 8 - 1), and some seq index uses all of its slots. slot_image is -1 exactly where slot_dest is -1; an image is one block or the two blocks of a slot pair, and different images have different ids.
All inputs are finite; a program needn't handle non-finite values.
Results may differ from a plain program's by a relative error of at most 0.035.
Values may be sent and summed in bfloat16 or wider, within the bound.
A program may use at most 128 MiB of HBM per device.

v0:
```python
import jax
import jax.numpy as jnp
from jax import lax
from jax.sharding import PartitionSpec as P

HDIM = 64
BLK = 256
BLK_DEV = 8


EPSILON = 1e-06
RATE_SCALE = 0.1


def norm_rows(values, gain_vector):
    widened = values.astype(jnp.float32)
    factor = lax.rsqrt(jnp.mean(widened * widened, axis=-1, keepdims=True) + EPSILON)
    return (widened * factor * gain_vector).astype(jnp.bfloat16)


def attend_pair(pieces):
    query_rows, key_rows, value_rows, token_ids = pieces
    token_count = query_rows.shape[0]
    heads_here = query_rows.shape[1] // HDIM
    q_heads = query_rows.reshape(token_count, heads_here, HDIM)
    k_heads = key_rows.reshape(token_count, heads_here, HDIM)
    v_heads = value_rows.reshape(token_count, heads_here, HDIM)
    scores = jnp.einsum(
        "qhe,khe->hqk", q_heads, k_heads, preferred_element_type=jnp.float32
    ) * HDIM ** (-0.5)
    allowed = token_ids[:, None] == token_ids[None, :]
    scores = jnp.where(allowed[None], scores, -1e30)
    top_score = jnp.max(scores, axis=-1, keepdims=True)
    exp_scores = jnp.exp(scores - top_score)
    weights = (exp_scores / jnp.sum(exp_scores, axis=-1, keepdims=True)).astype(jnp.bfloat16)
    mixed_heads = jnp.einsum("hqk,khe->qhe", weights, v_heads, preferred_element_type=jnp.float32)
    return mixed_heads.astype(jnp.bfloat16).reshape(token_count, heads_here * HDIM)


def encode_blocks(full_rows, block_ids, enc_gain, w_qkv):
    normed = norm_rows(full_rows, enc_gain)
    query_rows = jnp.dot(normed, w_qkv[0], preferred_element_type=jnp.float32).astype(jnp.bfloat16)
    key_rows = jnp.dot(normed, w_qkv[1], preferred_element_type=jnp.float32).astype(jnp.bfloat16)
    value_rows = jnp.dot(normed, w_qkv[2], preferred_element_type=jnp.float32).astype(jnp.bfloat16)
    columns = query_rows.shape[1]
    span = 2 * BLK
    pair_count = full_rows.shape[0] // span
    token_ids = jnp.repeat(block_ids, BLK, total_repeat_length=pair_count * span).reshape(
        pair_count, span
    )
    attended = lax.map(
        attend_pair,
        (
            query_rows.reshape(pair_count, span, columns),
            key_rows.reshape(pair_count, span, columns),
            value_rows.reshape(pair_count, span, columns),
            token_ids,
        ),
    )
    return attended.reshape(pair_count * span, columns)


def route_matrix(destinations, seq_count, room):
    slot_count = destinations.shape[0]
    target_seq = jnp.where(destinations >= 0, destinations // BLK_DEV, -1)
    position = jnp.arange(slot_count)
    earlier = position[None, :] < position[:, None]
    same_target = (target_seq[None, :] == target_seq[:, None]) & earlier
    ranking = jnp.sum(same_target.astype(jnp.int32), axis=1)
    bucket = jnp.where(destinations >= 0, target_seq * room + ranking, -1)
    return bucket[None, :] == jnp.arange(seq_count * room)[:, None]


def pack_rows(selection, payload):
    return jnp.dot(
        selection.astype(jnp.bfloat16), payload, preferred_element_type=jnp.float32
    ).astype(jnp.bfloat16)


def pack_index(selection, indices):
    return jnp.sum(jnp.where(selection, indices[None, :] + 1, 0), axis=1).astype(jnp.int32) - 1


def place_matrix(arrived, seq_index):
    local_block = arrived - seq_index * BLK_DEV
    return (local_block[None, :] == jnp.arange(BLK_DEV)[:, None]) & (arrived >= 0)[None, :]


def renorm(updated, initial):
    target_norm = jnp.sqrt(jnp.sum(initial * initial, axis=1, keepdims=True))
    return (
        updated
        * target_norm
        * lax.rsqrt(jnp.sum(updated * updated, axis=1, keepdims=True) + EPSILON)
    )


def on_device(
    patches,
    slot_image,
    slot_dest,
    enc_gain,
    w_qkv,
    w_out,
    fast_gain,
    w_fast,
    w_rate,
    fast_gate_up,
    fast_down,
):
    seq_count = lax.axis_size("seq")
    seq_index = lax.axis_index("seq")
    head_index = lax.axis_index("head")
    width = w_out.shape[0]
    slot_count = slot_dest.shape[0]
    room = 2 * ((BLK_DEV + seq_count - 1) // seq_count)
    patch_blocks = patches.reshape(slot_count, BLK, patches.shape[1])
    own_columns = lax.dynamic_slice_in_dim(patch_blocks, head_index * width, width, 2).reshape(
        slot_count, BLK * width
    )
    selection = route_matrix(slot_dest, seq_count, room)
    sent_dest = pack_index(selection, slot_dest)
    got_own, arrived, got_ids = (
        lax.all_to_all(
            pack_rows(selection, own_columns), "seq", split_axis=0, concat_axis=0, tiled=True
        ),
        lax.all_to_all(sent_dest, "seq", split_axis=0, concat_axis=0, tiled=True),
        lax.all_to_all(
            pack_index(selection, slot_image), "seq", split_axis=0, concat_axis=0, tiled=True
        ),
    )
    placing = place_matrix(arrived, seq_index)
    view_own = pack_rows(placing, got_own)
    view_ids = pack_index(placing, got_ids)
    whole_rows = lax.all_gather(view_own.reshape(BLK_DEV * BLK, width), "head", axis=1, tiled=True)
    view_attn = encode_blocks(whole_rows, view_ids, enc_gain, w_qkv)
    partial_value = jnp.dot(view_attn, w_out, preferred_element_type=jnp.float32)
    head_mixed = lax.psum_scatter(
        partial_value.astype(jnp.bfloat16), "head", scatter_dimension=1, tiled=True
    ).astype(jnp.float32)
    embedded = (head_mixed + view_own.reshape(BLK_DEV * BLK, width).astype(jnp.float32)).astype(
        jnp.bfloat16
    )
    full_embedded = lax.all_gather(embedded, "head", axis=1, tiled=True)
    normed_fast = norm_rows(full_embedded, fast_gain)
    fast_query = jnp.dot(normed_fast, w_fast[0], preferred_element_type=jnp.float32).astype(
        jnp.bfloat16
    )
    fast_key = jnp.dot(normed_fast, w_fast[1], preferred_element_type=jnp.float32).astype(
        jnp.bfloat16
    )
    fast_value = jnp.dot(normed_fast, w_fast[2], preferred_element_type=jnp.float32).astype(
        jnp.bfloat16
    )
    token_total = embedded.shape[0] * seq_count
    rates = (
        RATE_SCALE
        * jax.nn.softplus(jnp.dot(normed_fast, w_rate, preferred_element_type=jnp.float32))
        * token_total ** (-0.5)
    )
    gate_init = fast_gate_up[0, 0]
    up_init = fast_gate_up[0, 1]
    down_init = fast_down[0]
    gate_half = gate_init.astype(jnp.bfloat16)
    up_half = up_init.astype(jnp.bfloat16)
    down_half = down_init.astype(jnp.bfloat16)
    key_gate = jnp.dot(fast_key, gate_half, preferred_element_type=jnp.float32)
    key_up = jnp.dot(fast_key, up_half, preferred_element_type=jnp.float32)
    hidden_key = (jax.nn.silu(key_gate) * key_up).astype(jnp.bfloat16)
    out_grad = (-rates * fast_value.astype(jnp.float32)).astype(jnp.bfloat16)
    grad_down = jnp.einsum("th,tf->hf", hidden_key, out_grad, preferred_element_type=jnp.float32)
    hidden_grad = jnp.dot(out_grad, down_half.T, preferred_element_type=jnp.float32)
    sigmoid_gate = jax.nn.sigmoid(key_gate)
    gate_grad = (
        hidden_grad * key_up * sigmoid_gate * (1.0 + key_gate * (1.0 - sigmoid_gate))
    ).astype(jnp.bfloat16)
    up_grad = (hidden_grad * jax.nn.silu(key_gate)).astype(jnp.bfloat16)
    grad_gate = jnp.einsum("tf,th->fh", fast_key, gate_grad, preferred_element_type=jnp.float32)
    grad_up = jnp.einsum("tf,th->fh", fast_key, up_grad, preferred_element_type=jnp.float32)
    grad_gate, grad_up, grad_down = (
        lax.psum(grad_gate.astype(jnp.bfloat16), "seq").astype(jnp.float32),
        lax.psum(grad_up.astype(jnp.bfloat16), "seq").astype(jnp.float32),
        lax.psum(grad_down.astype(jnp.bfloat16), "seq").astype(jnp.float32),
    )
    new_gate = renorm(gate_init - grad_gate, gate_init)
    new_up = renorm(up_init - grad_up, up_init)
    new_down = renorm(down_init - grad_down, down_init)
    applied_gate = new_gate.astype(jnp.bfloat16)
    applied_up = new_up.astype(jnp.bfloat16)
    applied_down = new_down.astype(jnp.bfloat16)
    query_gate = jnp.dot(fast_query, applied_gate, preferred_element_type=jnp.float32)
    query_up = jnp.dot(fast_query, applied_up, preferred_element_type=jnp.float32)
    query_hidden = (jax.nn.silu(query_gate) * query_up).astype(jnp.bfloat16)
    fast_out = jnp.dot(query_hidden, applied_down, preferred_element_type=jnp.float32)
    return (embedded.astype(jnp.float32) + fast_out).astype(jnp.bfloat16)


def solution(mesh):
    in_specs = (
        P("seq", None),
        P("seq"),
        P("seq"),
        P(),
        P(None, None, "head"),
        P("head", None),
        P(),
        P(None, None, "head"),
        P(None, "head"),
        P("head", None, None, None),
        P("head", None, None),
    )
    out_specs = P("seq", "head")
    return jax.shard_map(
        on_device, mesh=mesh, in_specs=in_specs, out_specs=out_specs, check_vma=False
    )
```

profile of v0, /device:TPU:24, one launch (start us, length us, event | category | flops | bytes accessed | tf_op | source)
XLA Modules:
  0.0 308.6 jit_solution(212847610619158784)
XLA Ops:
  6.5 0.7 broadcast_add_fusion.3
  7.2 0.7 broadcast_add_fusion.4
  8.1 0.7 compare_select_fusion.4
  8.9 0.7 sub.54
  9.6 6.0 %all-to-all-start = ((s32[8,2,1]{1,2,0:T(1,128)}), s32[8,2,1]{1,2,0:T(1,128)S(1)}, u32[]{:S(2)}, u32[]{:S(2)}) async-start(s32[8,2,1]{1,2,0:T(1,128)} %bitcast.6), calls=%async_computation | async-start | bytes 8192 | tf_op jit(solution)/shard_map/all_to_all | solution.py:127
  15.6 2.9 constant_dynamic-slice_fusion.4
  18.5 3.2 %reshape.274 = bf16[16,49152]{1,0:T(8,128)(2,1)} reshape(bf16[16,256,192]{2,1,0:T(8,128)(2,1)S(1)} %constant_dynamic-slice_fusion.4) | data formatting | bytes 3145728 | tf_op jit(solution)/shard_map/reshape | solution.py:118
  21.7 2.0 convolution_convert_fusion
  23.7 1.9 all_to_all.17
  25.6 6.0 %all-to-all-start.1 = ((bf16[8,2,49152]{2,1,0:T(2,128)(2,1)}), bf16[8,2,49152]{2,1,0:T(2,128)(2,1)S(1)}, u32[]{:S(2)}, u32[]{:S(2)}) async-start(bf16[8,2,49152]{2,1,0:T(2,128)(2,1)} %all_to_all.17), calls=%async_computation.1 | async-start | bytes 3145728 | tf_op jit(solution)/shard_map/all_to_all | solution.py:124
  31.8 33.7 %all-to-all-done.1 = bf16[8,2,49152]{2,1,0:T(2,128)(2,1)S(1)} async-done(((bf16[8,2,49152]{2,1,0:T(2,128)(2,1)}), bf16[8,2,49152]{2,1,0:T(2,128)(2,1)S(1)}, u32[]{:S(2)}, u32[]{:S(2)}) %all-to-all-start.1) | async-done | bytes 1572896 | tf_op jit(solution)/shard_map/all_to_all | solution.py:124
  65.5 0.6 all_to_all.19
  66.3 1.2 convolution_convert_fusion.1
  67.5 2.3 reshape.275
  69.8 1.2 copy.34
  71.1 0.7 sub.59
  71.8 6.2 %all-to-all-start.2 = ((s32[8,2,1]{1,2,0:T(1,128)}), s32[8,2,1]{1,2,0:T(1,128)S(1)}, u32[]{:S(2)}, u32[]{:S(2)}) async-start(s32[8,2,1]{1,2,0:T(1,128)} %bitcast.9), calls=%async_computation.2 | async-start | bytes 8192 | tf_op jit(solution)/shard_map/all_to_all | solution.py:128
  77.9 3.2 %all-to-all-done.2 = s32[8,2,1]{1,2,0:T(1,128)S(1)} async-done(((s32[8,2,1]{1,2,0:T(1,128)}), s32[8,2,1]{1,2,0:T(1,128)S(1)}, u32[]{:S(2)}, u32[]{:S(2)}) %all-to-all-start.2) | async-done | bytes 96 | tf_op jit(solution)/shard_map/all_to_all | solution.py:128
  81.4 0.7 fusion.74
  82.1 5.0 %select_select_fusion = s32[2048]{0:T(1024)S(1)} fusion(pred[2048]{0:T(1024)(128)(4,1)S(1)} %copy-done.21, pred[2048]{0:T(1024)(128)(4,1)S(1)} %copy-done.20, pred[2048]{0:T(1024)(128)(4,1)S(1)} %copy-done.19, pred[2048]{0:T(1024)(128)(4,1)S(1)} %copy-done.18, pred[2048]{0:T(1024)(128)(4,1)S(1)} %copy-done.17, pred[2048]{0:T(1024)(128)(4,1)S(1)} %copy-done.16, ...), kind=kLoop, calls=%fused_computation.103 | loop fusion | flops 14336 | bytes 22560 | tf_op jit(solution)/shard_map/jit(_take)/gather | solution.py:48
  87.1 13.4 %all-gather.3.cloned.1.call-done = bf16[2048,768]{0,1:T(8,128)(2,1)} async-done(((bf16[2048,192]{0,1:T(8,128)(2,1)}), bf16[2048,768]{0,1:T(8,128)(2,1)}) %all-gather.3.cloned.1.call-update) | async-done | bytes 3145744 | tf_op jit(solution)/shard_map/all_gather | solution.py:135
  100.5 2.7 fusion.11
  103.4 1.1 convolution_convert_fusion.7
  104.5 1.1 convolution_convert_fusion.6
  105.7 1.1 convolution_convert_fusion.8
  106.9 25.0 %while.11 = (s32[]{:T(128)}, bf16[4,512,192]{1,2,0:T(8,128)(2,1)}, bf16[4,512,192]{1,2,0:T(8,128)(2,1)S(1)}, s32[4,512]{1,0:T(4,128)S(1)}, bf16[4,512,192]{1,2,0...) while((s32[]{:T(128)}, bf16[4,512,192]{1,2,0:T(8,128)(2,1)}, ...), condition=%wide.region_8.9_spmd, body=%wide.region_5.8_spmd.sunk | while | flops 206406144 | bytes 9193573 | solution.py:51
  106.9 0.2 broadcast_compare_fusion.2
  107.2 3.0 fusion.111
  110.2 2.3 fusion.112
  112.5 0.7 constant_dynamic-update-slice_fusion.2
  113.5 3.0 fusion.111
  116.4 2.3 fusion.112
  118.7 0.7 constant_dynamic-update-slice_fusion.2
  119.7 3.0 fusion.111
  122.7 2.3 fusion.112
  125.0 0.7 constant_dynamic-update-slice_fusion.2
  125.9 3.0 fusion.111
  128.9 2.3 fusion.112
  131.2 0.7 constant_dynamic-update-slice_fusion.2
  131.9 1.2 copy.45
  133.1 2.7 convolution_convert_fusion.2
  135.9 38.0 %reduce-scatter.2.cloned.1.call-done = bf16[2048,192]{0,1:T(8,128)(2,1)} async-done(((bf16[2048,768]{0,1:T(8,128)(2,1)}), bf16[2048,192]{0,1:T(8,128)(2,1)}) %reduce-scatter.2.cloned.1.call-update) | async-done | bytes 786448 | tf_op jit(solution)/shard_map/reduce_scatter | solution.py:138
  173.9 2.3 add_convert_fusion
  176.2 0.3 all-reduce.3.cloned.1.call-start
  176.4 28.4 %all-gather.5.cloned.1.call-done = bf16[2048,768]{0,1:T(8,128)(2,1)} async-done(((bf16[2048,192]{0,1:T(8,128)(2,1)}), bf16[2048,768]{0,1:T(8,128)(2,1)}) %all-gather.5.cloned.1.call-update) | async-done | bytes 3145744 | tf_op jit(solution)/shard_map/all_gather | solution.py:144
  204.8 2.7 fusion.14
  207.7 0.7 fusion.16
  208.4 0.4 copy-done.10
  208.8 0.8 convolution_convert_fusion.4
  209.7 0.3 copy-done.3
  209.9 0.8 fusion.46
  210.7 0.8 fusion.48
  211.5 0.5 fusion.78
  212.0 0.8 fusion.21
  212.9 0.7 fusion.75
  213.7 1.8 fusion.25
  215.5 2.1 fusion.27
  217.6 1.8 fusion.26
  219.4 2.6 convolution_convert_fusion.5
  222.1 69.4 %all-reduce.3.cloned.1.call-done = (bf16[192,384]{1,0:T(8,128)(2,1)}, bf16[192,384]{1,0:T(8,128)(2,1)}, bf16[384,192]{0,1:T(8,128)(2,1)}) async-done(((bf16[192,384]{1,0:T(8,128)(2,1)}, bf16[192,384]{1,0:T(8,128)(2,1)}, bf16[384,192]{0,1:T(8,128)(2,1)}), (bf16[192,384]{1,0:T(8,128)(2,1)}, bf16[192,384]{1,0:T(8,128)(2,1)}, bf16[384,192]{0,1:T(8,128)(2,1)})) %all-reduce.3.cloned.1.call-update) | async-done | bytes 442384 | tf_op jit(solution)/shard_map/psum | solution.py:181
  291.4 1.4 fusion.30
  292.9 1.1 fusion.31
  294.0 3.8 %fusion.45 = f32[2048,384]{1,0:T(8,128)} fusion(bf16[2048,192]{0,1:T(8,128)(2,1)} %convolution_convert_fusion.5, bf16[192,384]{1,0:T(8,128)(2,1)} %get-tuple-element.94, f32[1,2,192,384]{3,2,1,0:T(8,128)} %param.24, f32[192]{0:T(256)S(1)} %add_rsqrt_fusion.4, f32[192]{0:T(256)S(1)} %sqrt.24), kind=kOutput, calls=%fused_computation.89 | convolution fusion | flops 302358528 | bytes 4376064 | tf_op jit(solution)/shard_map/dot_general | solution.py:191
  297.8 4.3 %fusion.18 = bf16[2048,192]{0,1:T(8,128)(2,1)} fusion(bf16[2048,192]{0,1:T(8,128)(2,1)S(1)} %copy-done.6, f32[2048,384]{1,0:T(8,128)} %fusion.45, bf16[2048,192]{0,1:T(8,128)(2,1)S(1)} %copy-done.7, bf16[192,384]{1,0:T(8,128)(2,1)S(1)} %copy-done.11, f32[1,2,192,384]{3,2,1,0:T(8,128)S(1)} %copy-done.4, bf16[384,192]{0,1:T(8,128)(2,1)S(1)} %copy-done.12, ...), kind=kOutput, calls=%fused_computation.39 | convolution fusion | flops 610615296 | bytes 6395904 | tf_op jit(solution)/shard_map/dot_general | solution.py:194
  (94 shorter events, 2.4 us)
Async XLA Ops:
  6.5 126.6 %copy-start = (bf16[192,768]{1,0:T(8,128)(2,1)S(1)}, bf16[192,768]{1,0:T(8,128)(2,1)}, u32[]{:S(2)}) copy-start(bf16[192,768]{1,0:T(8,128)(2,1)} %param.20) | copy-start | bytes 884740
  9.6 16.1 %all-to-all-start = ((s32[8,2,1]{1,2,0:T(1,128)}), s32[8,2,1]{1,2,0:T(1,128)S(1)}, u32[]{:S(2)}, u32[]{:S(2)}) async-start(s32[8,2,1]{1,2,0:T(1,128)} %bitcast.6), calls=%async_computation | async-start | bytes 8192 | tf_op jit(solution)/shard_map/all_to_all | solution.py:127
  25.6 39.9 %all-to-all-start.1 = ((bf16[8,2,49152]{2,1,0:T(2,128)(2,1)}), bf16[8,2,49152]{2,1,0:T(2,128)(2,1)S(1)}, u32[]{:S(2)}, u32[]{:S(2)}) async-start(bf16[8,2,49152]{2,1,0:T(2,128)(2,1)} %all_to_all.17), calls=%async_computation.1 | async-start | bytes 3145728 | tf_op jit(solution)/shard_map/all_to_all | solution.py:124
  31.6 68.9 %all-gather.3.cloned.1.call-start = ((), (), s32[]{:S(2)}) async-start(), calls=%async_computation.4 | async-start | bytes 3932160 | tf_op jit(solution)/shard_map/all_gather | solution.py:135
  66.2 15.9 %copy-start.15 = (pred[2048]{0:T(1024)(128)(4,1)S(1)}, pred[2048]{0:T(1024)(128)(4,1)}, u32[]{:S(2)}) copy-start(pred[2048]{0:T(1024)(128)(4,1)} %constant.200) | copy-start | bytes 6148
  66.2 15.9 %copy-start.16 = (pred[2048]{0:T(1024)(128)(4,1)S(1)}, pred[2048]{0:T(1024)(128)(4,1)}, u32[]{:S(2)}) copy-start(pred[2048]{0:T(1024)(128)(4,1)} %constant.199) | copy-start | bytes 6148
  66.2 15.9 %copy-start.17 = (pred[2048]{0:T(1024)(128)(4,1)S(1)}, pred[2048]{0:T(1024)(128)(4,1)}, u32[]{:S(2)}) copy-start(pred[2048]{0:T(1024)(128)(4,1)} %constant.198) | copy-start | bytes 6148
  66.2 15.9 %copy-start.18 = (pred[2048]{0:T(1024)(128)(4,1)S(1)}, pred[2048]{0:T(1024)(128)(4,1)}, u32[]{:S(2)}) copy-start(pred[2048]{0:T(1024)(128)(4,1)} %constant.197) | copy-start | bytes 6148
  66.2 15.9 %copy-start.19 = (pred[2048]{0:T(1024)(128)(4,1)S(1)}, pred[2048]{0:T(1024)(128)(4,1)}, u32[]{:S(2)}) copy-start(pred[2048]{0:T(1024)(128)(4,1)} %constant.196) | copy-start | bytes 6148
  66.2 15.9 %copy-start.20 = (pred[2048]{0:T(1024)(128)(4,1)S(1)}, pred[2048]{0:T(1024)(128)(4,1)}, u32[]{:S(2)}) copy-start(pred[2048]{0:T(1024)(128)(4,1)} %constant.195) | copy-start | bytes 6148
  66.2 15.9 %copy-start.21 = (pred[2048]{0:T(1024)(128)(4,1)S(1)}, pred[2048]{0:T(1024)(128)(4,1)}, u32[]{:S(2)}) copy-start(pred[2048]{0:T(1024)(128)(4,1)} %constant.194) | copy-start | bytes 6148
  69.8 33.4 %copy-start.22 = (bf16[3,768,192]{1,2,0:T(8,128)(2,1)S(1)}, bf16[3,768,192]{1,2,0:T(8,128)(2,1)}, u32[]{:S(2)}) copy-start(bf16[3,768,192]{1,2,0:T(8,128)(2,1)} %param.19) | copy-start | bytes 2654212
  69.8 33.4 %copy-start.23 = (f32[768]{0:T(1024)S(1)}, f32[768]{0:T(1024)}, u32[]{:S(2)}) copy-start(f32[768]{0:T(1024)} %param.18) | copy-start | bytes 9220
  71.8 9.4 %all-to-all-start.2 = ((s32[8,2,1]{1,2,0:T(1,128)}), s32[8,2,1]{1,2,0:T(1,128)S(1)}, u32[]{:S(2)}, u32[]{:S(2)}) async-start(s32[8,2,1]{1,2,0:T(1,128)} %bitcast.9), calls=%async_computation.2 | async-start | bytes 8192 | tf_op jit(solution)/shard_map/all_to_all | solution.py:128
  77.9 95.9 %reduce-scatter.2.cloned.1.call-start = ((), (), s32[]{:S(2)}) async-start(), calls=%async_computation.5 | async-start | bytes 3932160 | tf_op jit(solution)/shard_map/reduce_scatter | solution.py:138
  100.5 2.8 copy-start.5
  135.8 38.0 %copy-start.2 = (bf16[2048,192]{0,1:T(8,128)(2,1)S(1)}, bf16[2048,192]{0,1:T(8,128)(2,1)}, u32[]{:S(2)}) copy-start(bf16[2048,192]{0,1:T(8,128)(2,1)} %copy.34) | copy-start | bytes 2359300
  135.8 71.7 %copy-start.13 = (f32[768]{0:T(1024)S(1)}, f32[768]{0:T(1024)}, u32[]{:S(2)}) copy-start(f32[768]{0:T(1024)} %param.21) | copy-start | bytes 9220
  135.9 69.0 %all-gather.5.cloned.1.call-start = ((), (), s32[]{:S(2)}) async-start(), calls=%async_computation.6 | async-start | bytes 3932160 | tf_op jit(solution)/shard_map/all_gather | solution.py:144
  176.2 115.3 %all-reduce.3.cloned.1.call-start = ((), (), s32[]{:S(2)}) async-start(), calls=%async_computation.7 | async-start | bytes 884736 | tf_op jit(solution)/shard_map/psum | solution.py:181
  204.8 2.8 copy-start.1
  207.7 1.2 copy-start.10
  208.8 1.1 copy-start.3
  210.7 0.8 copy-start.14
  212.0 1.0 copy-start.8
  222.1 75.7 %copy-start.4 = (f32[1,2,192,384]{3,2,1,0:T(8,128)S(1)}, f32[1,2,192,384]{3,2,1,0:T(8,128)}, u32[]{:S(2)}) copy-start(f32[1,2,192,384]{3,2,1,0:T(8,128)} %param.24) | copy-start | bytes 1769476
  222.1 75.7 %copy-start.6 = (bf16[2048,192]{0,1:T(8,128)(2,1)S(1)}, bf16[2048,192]{0,1:T(8,128)(2,1)}, u32[]{:S(2)}) copy-start(bf16[2048,192]{0,1:T(8,128)(2,1)} %add_convert_fusion) | copy-start | bytes 2359300
  222.1 75.7 %copy-start.7 = (bf16[2048,192]{0,1:T(8,128)(2,1)S(1)}, bf16[2048,192]{0,1:T(8,128)(2,1)}, u32[]{:S(2)}) copy-start(bf16[2048,192]{0,1:T(8,128)(2,1)} %convolution_convert_fusion.5) | copy-start | bytes 2359300
  222.1 75.7 %copy-start.9 = (f32[1,384,192]{1,2,0:T(8,128)S(1)}, f32[1,384,192]{1,2,0:T(8,128)}, u32[]{:S(2)}) copy-start(f32[1,384,192]{1,2,0:T(8,128)} %param.25) | copy-start | bytes 884740
  291.4 6.3 %copy-start.11 = (bf16[192,384]{1,0:T(8,128)(2,1)S(1)}, bf16[192,384]{1,0:T(8,128)(2,1)}, u32[]{:S(2)}) copy-start(bf16[192,384]{1,0:T(8,128)(2,1)} %get-tuple-element.95) | copy-start | bytes 442372
  291.4 6.3 %copy-start.12 = (bf16[384,192]{0,1:T(8,128)(2,1)S(1)}, bf16[384,192]{0,1:T(8,128)(2,1)}, u32[]{:S(2)}) copy-start(bf16[384,192]{0,1:T(8,128)(2,1)} %get-tuple-element.96) | copy-start | bytes 442372
Sparse Core Ops, SparseCore 0:
  71.2 29.2 all-gather.2
  136.0 37.8 reduce-scatter.1
  176.3 28.5 all-gather.4
  219.6 71.8 all-reduce.2
where the time goes:
time: 312 us; the launch traced here: 309 us
  waiting for transfers between devices  186 us (60%)
  matrix products  51 us (16%)
  local copies, waits for them, and re-layouts  20.1 us (6%)
  other arithmetic  19.3 us (6%)
  starting transfers between devices  18.5 us (6%)
  between operations  13.5 us (4%)
    psum x1, waiting for transfers between devices, on_device(): lax.psum(grad_gate.astype(jnp.bfloat16), 'seq').astype(jnp.float32)  69.4 us
    reduce_scatter x1, waiting for transfers between devices, on_device(): lax.psum_scatter(partial_value.astype(jnp.bfloat16), 'head', scatter_dime...  38 us
    all_to_all x1, waiting for transfers between devices, on_device(): lax.all_to_all(pack_rows(selection, own_columns), 'seq', split_axis=0, co...  33.7 us
    all_gather x1, waiting for transfers between devices, on_device(): full_embedded = lax.all_gather(embedded, 'head', axis=1, tiled=True)  28.4 us
    all_gather x1, waiting for transfers between devices, on_device(): lax.all_gather(view_own.reshape(BLK_DEV * BLK, width), 'head', axis=1, ti...  13.4 us
    sub x4, matrix products, attend_pair(): exp_scores = jnp.exp(scores - top_score)  11.9 us
    dot_general x4, matrix products, attend_pair(): jnp.einsum('hqk,khe->qhe', weights, v_heads, preferred_element_type=jnp.f...  9.15 us
  transfers between devices with their start and end apart: 7, of which 6 were waited for; matrix products, arithmetic and copies ran while one was open for 6% of the time, Pallas kernels for 0%

commit v1 on v0

v1 whole, which is shorter than its diff:
```python
import functools

import jax
import jax.numpy as jnp
from jax import lax
from jax.experimental import pallas as pl
from jax.experimental.pallas import tpu as pltpu
from jax.sharding import PartitionSpec as P

HDIM = 64
BLK = 256
BLK_DEV = 8
PAIR = 2 * BLK
EPSILON = 1e-06
RATE_SCALE = 0.1
LANES = 128
MESH = pl.DeviceIdType.MESH
VMEM = pl.BlockSpec(memory_space=pltpu.VMEM)
NT = (((1,), (1,)), ((), ()))


def remote(src, dst, send, recv, device):
    return pltpu.make_async_remote_copy(
        src_ref=src, dst_ref=dst, send_sem=send, recv_sem=recv, device_id=device, device_id_type=MESH
    )


def comm_params(number):
    return pltpu.CompilerParams(
        collective_id=number, has_side_effects=True, vmem_limit_bytes=56 * 1024 * 1024
    )


def greet(devices):
    barrier = pltpu.get_barrier_semaphore()
    for device in devices:
        pl.semaphore_signal(barrier, inc=1, device_id=device, device_id_type=MESH)
    pl.semaphore_wait(barrier, len(devices))


def others(axis_size, me):
    return [lax.rem(me + step, axis_size) for step in range(1, axis_size)]


def head_pals(head_count, head):
    partner = head + 1 - 2 * lax.rem(head, 2)
    peer = lax.rem(head + head_count // 2, head_count)
    return partner, peer


def entry_kernel(n, nh, x_ref, m_ref, w_ref, ox, om, ow, sx, rx, sm, rm, sw, rw):
    seq, head = lax.axis_index("seq"), lax.axis_index("head")
    partner, peer = head_pals(nh, head)
    across = lax.rem(partner + nh // 2, nh)
    targets = others(n, seq)
    greet([(seq, partner), (seq, peer)] + [(to, head) for to in targets])
    to_peer = remote(w_ref, ow.at[:, head], sw.at[0], rw.at[0], (seq, peer))
    to_partner = remote(w_ref, ow.at[:, head], sw.at[1], rw.at[1], (seq, partner))
    to_peer.start()
    to_partner.start()
    copies = []
    for step, to in enumerate(targets):
        copies.append(remote(m_ref.at[to], om.at[seq], sm.at[step], rm.at[step], (to, head)))
        copies.append(remote(x_ref.at[to], ox.at[seq], sx.at[step], rx.at[step], (to, head)))
    for copy in copies:
        copy.start()
    ox[seq] = x_ref[seq]
    om[seq] = m_ref[seq]
    for part in range(w_ref.shape[0]):
        ow[part, head] = w_ref[part]
    to_peer.wait_recv()
    forward = remote(ow.at[:, peer], ow.at[:, peer], sw.at[2], rw.at[2], (seq, partner))
    forward.start()
    to_peer.wait_send()
    to_partner.wait()
    for copy in copies:
        copy.wait()
    forward.wait()


def enter(rows, meta, weights, n, nh):
    dma = pltpu.SemaphoreType.DMA
    return pl.pallas_call(
        functools.partial(entry_kernel, n, nh),
        out_shape=(
            jax.ShapeDtypeStruct(rows.shape, rows.dtype),
            jax.ShapeDtypeStruct(meta.shape, meta.dtype),
            jax.ShapeDtypeStruct(
                (weights.shape[0], nh) + weights.shape[1:], weights.dtype
            ),
        ),
        in_specs=[VMEM] * 3,
        out_specs=(VMEM,) * 3,
        scratch_shapes=[
            dma((n - 1,)), dma((n - 1,)), dma((n - 1,)), dma((n - 1,)), dma((3,)), dma((3,)),
        ],
        compiler_params=comm_params(1),
        name="entry_exchange",
    )(rows, meta, weights)


def swap_kernel(nh, x_ref, o_ref, send, recv):
    seq, head = lax.axis_index("seq"), lax.axis_index("head")
    targets = others(nh, head)
    greet([(seq, to) for to in targets])
    copies = [
        remote(x_ref.at[to], o_ref.at[head], send.at[step], recv.at[step], (seq, to))
        for step, to in enumerate(targets)
    ]
    for copy in copies:
        copy.start()
    o_ref[head] = x_ref[head]
    for copy in copies:
        copy.wait()


def head_swap(x, nh):
    dma = pltpu.SemaphoreType.DMA
    return pl.pallas_call(
        functools.partial(swap_kernel, nh),
        out_shape=jax.ShapeDtypeStruct(x.shape, x.dtype),
        in_specs=[VMEM],
        out_specs=VMEM,
        scratch_shapes=[dma((nh - 1,)), dma((nh - 1,))],
        compiler_params=comm_params(2),
        name="head_swap",
    )(x)


def gather_kernel(nh, x_ref, o_ref, send, recv):
    seq, head = lax.axis_index("seq"), lax.axis_index("head")
    partner, peer = head_pals(nh, head)
    greet([(seq, partner), (seq, peer)])
    to_peer = remote(x_ref, o_ref.at[head], send.at[0], recv.at[0], (seq, peer))
    to_partner = remote(x_ref, o_ref.at[head], send.at[1], recv.at[1], (seq, partner))
    to_peer.start()
    to_partner.start()
    o_ref[head] = x_ref[...]
    to_peer.wait_recv()
    forward = remote(o_ref.at[peer], o_ref.at[peer], send.at[2], recv.at[2], (seq, partner))
    forward.start()
    to_peer.wait_send()
    to_partner.wait()
    forward.wait()


def head_gather(x, nh):
    dma = pltpu.SemaphoreType.DMA
    return pl.pallas_call(
        functools.partial(gather_kernel, nh),
        out_shape=jax.ShapeDtypeStruct((nh,) + x.shape, x.dtype),
        in_specs=[VMEM],
        out_specs=VMEM,
        scratch_shapes=[dma((3,)), dma((3,))],
        compiler_params=comm_params(3),
        name="head_gather",
    )(x)


def sum_kernel(n, x_ref, o_ref, held, send, recv, send_b, recv_b):
    seq, head = lax.axis_index("seq"), lax.axis_index("head")
    targets = others(n, seq)
    greet([(to, head) for to in targets])
    copies = [
        remote(x_ref.at[to], held.at[step], send.at[step], recv.at[step], (to, head))
        for step, to in enumerate(targets)
    ]
    for copy in copies:
        copy.start()
    total = x_ref[seq].astype(jnp.float32)
    for step, copy in enumerate(copies):
        copy.wait()
        total = total + held[step].astype(jnp.float32)
    o_ref[seq] = total.astype(o_ref.dtype)
    copies = [
        remote(o_ref.at[seq], o_ref.at[seq], send_b.at[step], recv_b.at[step], (to, head))
        for step, to in enumerate(targets)
    ]
    for copy in copies:
        copy.start()
    for copy in copies:
        copy.wait()


def seq_sum(x, n):
    dma = pltpu.SemaphoreType.DMA
    return pl.pallas_call(
        functools.partial(sum_kernel, n),
        out_shape=jax.ShapeDtypeStruct(x.shape, x.dtype),
        in_specs=[VMEM],
        out_specs=VMEM,
        scratch_shapes=[
            pltpu.VMEM((n - 1,) + x.shape[1:], x.dtype),
            dma((n - 1,)), dma((n - 1,)), dma((n - 1,)), dma((n - 1,)),
        ],
        compiler_params=comm_params(4),
        name="gradient_sum",
    )(x)


def pick_kernel(index_ref, x_ref, o_ref):
    o_ref[...] = x_ref[...]


def pick_blocks(x, index):
    block = (1,) + x.shape[1:]
    return pl.pallas_call(
        pick_kernel,
        out_shape=jax.ShapeDtypeStruct(index.shape + x.shape[1:], x.dtype),
        grid_spec=pltpu.PrefetchScalarGridSpec(
            num_scalar_prefetch=1,
            grid=index.shape,
            in_specs=[pl.BlockSpec(block, lambda i, index: (index[i], 0, 0))],
            out_specs=pl.BlockSpec(block, lambda i, index: (i, 0, 0)),
        ),
        name="pick_blocks",
    )(index, x)


def encode_kernel(flag_ref, x_ref, w_ref, gain_ref, o_ref, q_ref, k_ref, v_ref, a_ref):
    width = x_ref.shape[1]
    wide = x_ref[...].astype(jnp.float32)
    factor = lax.rsqrt(jnp.mean(wide * wide, axis=-1, keepdims=True) + EPSILON)
    normed = (wide * factor * gain_ref[...]).astype(jnp.bfloat16)

    def project(which):
        return lax.dot_general(
            normed, w_ref[which].reshape(width, width), NT, preferred_element_type=jnp.float32
        ).astype(jnp.bfloat16)

    q_ref[...] = project(0) * jnp.bfloat16(HDIM ** (-0.5))
    k_ref[...] = project(1)
    v_ref[...] = project(2)
    apart = jnp.where(flag_ref[0] > 0, 0.0, -1e30).astype(jnp.float32)
    key_block = lax.broadcasted_iota(jnp.int32, (1, PAIR), 1) // BLK
    first = lax.broadcasted_iota(jnp.int32, (BLK, LANES), 1) < HDIM

    def slab(index, carry):
        columns = pl.ds(pl.multiple_of(index * LANES, LANES), LANES)
        keys = k_ref[:, columns]
        values = v_ref[:, columns]
        for block in range(2):
            rows = pl.ds(block * BLK, BLK)
            bias = jnp.where(key_block == block, 0.0, apart)
            query = q_ref[rows, columns]
            halves = []
            for half in range(2):
                chosen = first if half == 0 else jnp.logical_not(first)
                own = jnp.where(chosen, query, jnp.zeros_like(query))
                scores = lax.dot_general(own, keys, NT, preferred_element_type=jnp.float32) + bias
                top = jnp.max(scores, axis=-1, keepdims=True)
                weights = jnp.exp(scores - top)
                total = jnp.sum(weights, axis=-1, keepdims=True)
                mixed = jnp.dot(
                    weights.astype(jnp.bfloat16), values, preferred_element_type=jnp.float32
                )
                halves.append(mixed * (1.0 / total))
            a_ref[rows, columns] = jnp.where(first, halves[0], halves[1]).astype(jnp.bfloat16)
        return carry

    lax.fori_loop(0, width // LANES, slab, 0)
    mixed = jnp.dot(a_ref[...], w_ref[3].reshape(width, width), preferred_element_type=jnp.float32)
    o_ref[...] = (x_ref[...].astype(jnp.float32) + mixed).astype(jnp.bfloat16)


def encode(flag, rows, weights, gain):
    return pl.pallas_call(
        encode_kernel,
        out_shape=jax.ShapeDtypeStruct(rows.shape, rows.dtype),
        in_specs=[pl.BlockSpec(memory_space=pltpu.SMEM), VMEM, VMEM, VMEM],
        out_specs=VMEM,
        scratch_shapes=[pltpu.VMEM(rows.shape, jnp.bfloat16)] * 4,
        compiler_params=pltpu.CompilerParams(vmem_limit_bytes=56 * 1024 * 1024),
        name="encode_pair",
    )(flag, rows, weights, gain)


def norm_rows(values, gain_vector):
    widened = values.astype(jnp.float32)
    factor = lax.rsqrt(jnp.mean(widened * widened, axis=-1, keepdims=True) + EPSILON)
    return (widened * factor * gain_vector).astype(jnp.bfloat16)


def renorm(updated, initial, axis):
    target_norm = jnp.sqrt(jnp.sum(initial * initial, axis=axis, keepdims=True))
    return (
        updated
        * target_norm
        * lax.rsqrt(jnp.sum(updated * updated, axis=axis, keepdims=True) + EPSILON)
    )


def to_tiles(gradient, n):
    rows, columns = gradient.shape
    flat = jnp.concatenate(
        [gradient[:, c : c + LANES] for c in range(0, columns, LANES)], axis=0
    )
    chunk = 16 * (-(-flat.shape[0] // (16 * n)))
    return jnp.pad(flat, ((0, chunk * n - flat.shape[0]), (0, 0))).reshape(n, chunk, LANES)


def from_tiles(tiles, rows, columns):
    flat = tiles.reshape(-1, LANES)
    return jnp.concatenate(
        [flat[c * rows : (c + 1) * rows] for c in range(columns // LANES)], axis=1
    )


def on_device(
    patches,
    slot_image,
    slot_dest,
    enc_gain,
    w_qkv,
    w_out,
    fast_gain,
    w_fast,
    w_rate,
    fast_gate_up,
    fast_down,
):
    n = lax.axis_size("seq")
    nh = lax.axis_size("head")
    head = lax.axis_index("head")
    width = w_out.shape[0]
    model = patches.shape[1]
    part = PAIR // nh
    shard_pairs = BLK_DEV // 2

    first_dest = slot_dest[0::2]
    same_image = (slot_image[0::2] == slot_image[1::2]).astype(jnp.int32)
    pair_dest = first_dest // 2
    goes = (pair_dest[None, :] // shard_pairs == jnp.arange(n)[:, None]) & (first_dest >= 0)[None, :]
    has = jnp.any(goes, axis=1)
    offset = head * part
    slot = 2 * jnp.arange(first_dest.shape[0]) + (first_dest + offset // BLK) % 2
    start = (slot * BLK + offset % BLK) // part
    send_index = jnp.sum(jnp.where(goes, start[None, :], 0), axis=1).astype(jnp.int32)
    code = jnp.sum(
        jnp.where(goes, (2 * (pair_dest % shard_pairs) + same_image)[None, :], 0), axis=1
    )
    code = jnp.where(has, code, -1).astype(jnp.int32)
    meta = jnp.broadcast_to(code[:, None, None], (n, 8, LANES))
    sending = pick_blocks(patches.reshape(-1, part, model), send_index)
    weights = jnp.concatenate([jnp.swapaxes(w_qkv, 1, 2), w_out[None]], axis=0)
    arrived, codes, full_weights = enter(sending, meta, weights, n, nh)
    codes = codes[:, 0, 0]
    source = (codes[None, :] >= 0) & (codes[None, :] // 2 == jnp.arange(shard_pairs)[:, None])
    source_index = jnp.sum(jnp.where(source, jnp.arange(n)[None, :], 0), axis=1).astype(jnp.int32)
    same = jnp.sum(
        jnp.where((codes >= 0) & (codes // 2 == head), codes % 2, 0)
    ).astype(jnp.int32)
    own_pair = head_swap(pick_blocks(arrived, source_index), nh).reshape(PAIR, model)
    own_embedded = encode(same.reshape(1), own_pair, full_weights, enc_gain[None, :])
    full_embedded = head_gather(own_embedded, nh).reshape(nh * PAIR, model)
    embedded = lax.dynamic_slice_in_dim(full_embedded, head * width, width, 1)

    normed_fast = norm_rows(full_embedded, fast_gain)
    fast_query = jnp.dot(normed_fast, w_fast[0], preferred_element_type=jnp.float32).astype(
        jnp.bfloat16
    )
    fast_key = jnp.dot(normed_fast, w_fast[1], preferred_element_type=jnp.float32).astype(
        jnp.bfloat16
    )
    fast_value = jnp.dot(normed_fast, w_fast[2], preferred_element_type=jnp.float32).astype(
        jnp.bfloat16
    )
    token_total = embedded.shape[0] * n
    rates = (
        RATE_SCALE
        * jax.nn.softplus(jnp.dot(normed_fast, w_rate, preferred_element_type=jnp.float32))
        * token_total ** (-0.5)
    )
    gate_init = fast_gate_up[0, 0]
    up_init = fast_gate_up[0, 1]
    down_init = fast_down[0]
    gate_half = gate_init.astype(jnp.bfloat16)
    up_half = up_init.astype(jnp.bfloat16)
    down_half = down_init.astype(jnp.bfloat16)
    key_gate = jnp.dot(fast_key, gate_half, preferred_element_type=jnp.float32)
    key_up = jnp.dot(fast_key, up_half, preferred_element_type=jnp.float32)
    sigmoid_gate = jax.nn.sigmoid(key_gate)
    hidden_key = (key_gate * sigmoid_gate * key_up).astype(jnp.bfloat16)
    out_grad = (-rates * fast_value.astype(jnp.float32)).astype(jnp.bfloat16)
    grad_down = jnp.einsum("tf,th->fh", out_grad, hidden_key, preferred_element_type=jnp.float32)
    hidden_grad = jnp.dot(out_grad, down_half.T, preferred_element_type=jnp.float32)
    gate_grad = (
        hidden_grad * key_up * sigmoid_gate * (1.0 + key_gate * (1.0 - sigmoid_gate))
    ).astype(jnp.bfloat16)
    up_grad = (hidden_grad * key_gate * sigmoid_gate).astype(jnp.bfloat16)
    grad_gate = jnp.einsum("tf,th->fh", fast_key, gate_grad, preferred_element_type=jnp.float32)
    grad_up = jnp.einsum("tf,th->fh", fast_key, up_grad, preferred_element_type=jnp.float32)
    gradient = jnp.concatenate([grad_gate, grad_up, grad_down], axis=0).astype(jnp.bfloat16)
    hidden = gradient.shape[1]
    summed = from_tiles(seq_sum(to_tiles(gradient, n), n), 3 * width, hidden).astype(jnp.float32)
    new_gate = renorm(gate_init - summed[:width], gate_init, 1)
    new_up = renorm(up_init - summed[width : 2 * width], up_init, 1)
    new_down = renorm(down_init.T - summed[2 * width :], down_init.T, 0)
    applied_gate = new_gate.astype(jnp.bfloat16)
    applied_up = new_up.astype(jnp.bfloat16)
    applied_down = new_down.astype(jnp.bfloat16)
    query_gate = jnp.dot(fast_query, applied_gate, preferred_element_type=jnp.float32)
    query_up = jnp.dot(fast_query, applied_up, preferred_element_type=jnp.float32)
    query_hidden = (jax.nn.silu(query_gate) * query_up).astype(jnp.bfloat16)
    fast_out = jnp.dot(query_hidden, applied_down.T, preferred_element_type=jnp.float32)
    return (embedded.astype(jnp.float32) + fast_out).astype(jnp.bfloat16)


def solution(mesh):
    in_specs = (
        P("seq", None),
        P("seq"),
        P("seq"),
        P(),
        P(None, None, "head"),
        P("head", None),
        P(),
        P(None, None, "head"),
        P(None, "head"),
        P("head", None, None, None),
        P("head", None, None),
    )
    out_specs = P("seq", "head")
    return jax.shard_map(
        on_device, mesh=mesh, in_specs=in_specs, out_specs=out_specs, check_vma=False
    )
```

time: 312 us -> 172 us (0.55)
  waiting for transfers between devices: 186 us -> 0 us
  Pallas kernels: 0 us -> 134 us
  matrix products: 51 us -> 17.2 us
  starting transfers between devices: 18.5 us -> 0 us
  between operations: 13.5 us -> 0.27 us
  other arithmetic: 19.3 us -> 9.39 us
  local copies, waits for them, and re-layouts: 20.1 us -> 10.3 us
    pallas_call x0 -> x7, Pallas kernels: none -> 134 us  [the longest x1 40.6 us: enter(): pl.pallas_call(functools.partial(entry_kernel, n, nh), out_shape=(jax.Sha...]
    psum x1 -> x0, waiting for transfers between devices: 69.4 us -> none  [on_device(): lax.psum(grad_gate.astype(jnp.bfloat16), 'seq').astype(jnp.float32)]
    all_gather x2 -> x0, waiting for transfers between devices: 41.8 us -> none  [the longest x1 28.4 us: on_device(): full_embedded = lax.all_gather(embedded, 'head', axis=1, tiled=True)]
    reduce_scatter x1 -> x0, waiting for transfers between devices: 38 us -> none  [on_device(): lax.psum_scatter(partial_value.astype(jnp.bfloat16), 'head', scatter_dime...]
    all_to_all x3 -> x0, waiting for transfers between devices: 36.9 us -> none  [the longest x1 33.7 us: on_device(): lax.all_to_all(pack_rows(selection, own_columns), 'seq', split_axis=0, co...]
    dot_general x12 -> x2, matrix products: 24.4 us -> 5.48 us  [the longest x1 4.34 us: on_device(): jnp.dot(query_hidden, applied_down.T, preferred_element_type=jnp.float32)]
    all_to_all x3 -> x0, starting transfers between devices: 18.2 us -> none  [the longest x1 6.16 us: on_device(): lax.all_to_all(pack_index(selection, slot_image), 'seq', split_axis=0, co...]
    sub x4 -> x0, matrix products: 11.9 us -> none  [attend_pair(): exp_scores = jnp.exp(scores - top_score)]
  transfers between devices with their start and end apart: 7 -> 0, of which waited for: 6 -> 0; matrix products, arithmetic and copies ran while one was open for 6% -> 0% of each run, Pallas kernels for 0% -> 0%
where the time goes in v1:
time: 172 us
  Pallas kernels  134 us (78%)
  matrix products  17.2 us (10%)
  local copies, waits for them, and re-layouts  10.3 us (6%)
  other arithmetic  9.39 us (5%)
    pallas_call x1, Pallas kernels, enter(): pl.pallas_call(functools.partial(entry_kernel, n, nh), out_shape=(jax.Sha...  40.6 us
    pallas_call x1, Pallas kernels, seq_sum(): pl.pallas_call(functools.partial(sum_kernel, n), out_shape=jax.ShapeDtype...  31.4 us
    pallas_call x1, Pallas kernels, head_gather(): pl.pallas_call(functools.partial(gather_kernel, nh), out_shape=jax.ShapeD...  25 us
    pallas_call x1, Pallas kernels, encode(): pl.pallas_call(encode_kernel, out_shape=jax.ShapeDtypeStruct(rows.shape,...  15.2 us
    pallas_call x1, Pallas kernels, head_swap(): pl.pallas_call(functools.partial(swap_kernel, nh), out_shape=jax.ShapeDty...  12.6 us
    pallas_call x2, Pallas kernels, pick_blocks(): pl.pallas_call(pick_kernel, out_shape=jax.ShapeDtypeStruct(index.shape +...  9.67 us
    dot_general x1, matrix products, on_device(): jnp.dot(query_hidden, applied_down.T, preferred_element_type=jnp.float32)  4.34 us

profile of v1, /device:TPU:24, one launch (start us, length us, event | category | flops | bytes accessed | tf_op | source)
XLA Modules:
  0.0 171.5 jit_solution(10767262179962866567)
XLA Ops:
  0.0 0.0 copy-start
  0.0 0.8 slice.54
  0.8 0.1 fusion.42
  0.9 0.7 slice.56
  1.7 0.7 slice.55
  2.4 0.7 select_reduce_fusion
  3.1 1.3 broadcast_in_dim.67.gain_ref
  4.4 0.7 broadcast_in_dim.63.m_ref
  5.1 2.5 %pad_maximum_fusion.w_ref = bf16[4,192,768]{2,1,0:T(8,128)(2,1)} fusion(bf16[1,192,768]{2,1,0:T(8,128)(2,1)} %bitcast.90, bf16[3,192,768]{2,1,0:T(8,128)(2,1)} %bitcast.89), kind=kLoop, calls=%fused_computation.21 | loop fusion | flops 589824 | bytes 2359296 | tf_op jit(solution)/shard_map/concatenate | solution.py:345
  7.6 5.7 %pick_blocks.2.x_ref = bf16[8,128,768]{2,1,0:T(8,128)(2,1)} custom-call(s32[8]{0:T(128)} %get-tuple-element.18.index_ref, bf16[32,128,768]{2,1,0:T(8,128)(2,1)} %bitcast.85), custom_call_target="tpu_custom_call" | custom-call | tf_op jit(solution)/shard_map/pick_blocks/pallas_call | solution.py:207
  13.3 40.6 %entry_exchange.1 = (bf16[8,128,768]{2,1,0:T(8,128)(2,1)}, s32[8,8,128]{2,1,0:T(8,128)}, bf16[4,4,192,768]{3,2,1,0:T(8,128)(2,1)}) custom-call(bf16[8,128,768]{2,1,0:T(8,128)(2,1)} %pick_blocks.2.x_ref, s32[8,8,128]{2,1,0:T(8,128)} %broadcast_in_dim.63.m_ref, bf16[4,192,768]{2,1,0:T(8,128)(2,1)} %pad_maximum_fusion.w_ref), custom_call_target="tpu_custom_call" | custom-call | tf_op jit(solution)/shard_map/entry_exchange/pallas_call | solution.py:83
  53.9 1.0 slice_reduce_fusion
  54.9 0.7 fusion.48
  55.6 0.7 select_reduce_fusion.2.index_ref
  56.2 3.9 %pick_blocks.3.x_ref = bf16[4,128,768]{2,1,0:T(8,128)(2,1)} custom-call(s32[4]{0:T(128)} %select_reduce_fusion.2.index_ref, bf16[8,128,768]{2,1,0:T(8,128)(2,1)} %get-tuple-element.9.x_ref), custom_call_target="tpu_custom_call" | custom-call | tf_op jit(solution)/shard_map/pick_blocks/pallas_call | solution.py:207
  60.2 12.6 %head_swap.1 = bf16[4,128,768]{2,1,0:T(8,128)(2,1)} custom-call(bf16[4,128,768]{2,1,0:T(8,128)(2,1)} %pick_blocks.3.x_ref), custom_call_target="tpu_custom_call" | custom-call | tf_op jit(solution)/shard_map/head_swap/pallas_call | solution.py:119
  72.7 15.2 %encode_pair.1.x_ref = bf16[512,768]{1,0:T(8,128)(2,1)} custom-call(s32[1]{0:T(128)} %bitcast.3.flag_ref, bf16[512,768]{1,0:T(8,128)(2,1)} %bitcast.86, bf16[4,4,192,768]{3,2,1,0:T(8,128)(2,1)} %get-tuple-element.10.w_ref, f32[1,768]{1,0:T(1,128)} %broadcast_in_dim.67.gain_ref), custom_call_target="tpu_custom_call" | custom-call | tf_op jit(solution)/shard_map/encode_pair/pallas_call | solution.py:267
  87.9 25.0 %head_gather.1 = bf16[4,512,768]{2,1,0:T(8,128)(2,1)} custom-call(bf16[512,768]{1,0:T(8,128)(2,1)} %encode_pair.1.x_ref), custom_call_target="tpu_custom_call" | custom-call | tf_op jit(solution)/shard_map/head_gather/pallas_call | solution.py:149
  112.9 0.0 copy-start.1
  112.9 0.0 copy-start.5
  112.9 2.7 %fusion = f32[4,512]{1,0:T(4,128)S(1)} fusion(bf16[4,512,768]{2,1,0:T(8,128)(2,1)} %head_gather.1), kind=kLoop, calls=%fused_computation.2 | loop fusion | flops 4716544 | bytes 3153920 | tf_op jit(solution)/shard_map/reduce_sum | solution.py:280
  115.6 0.1 copy-done.1
  115.7 1.4 constant_dynamic-slice_fusion
  117.1 2.2 %copy.15 = bf16[2048,192]{0,1:T(8,128)(2,1)} copy(bf16[2048,192]{1,0:T(8,128)(2,1)} %constant_dynamic-slice_fusion) | data formatting | bytes 1572864
  119.3 0.0 copy-done.5
  119.3 0.8 fusion.2
  120.1 0.0 copy-start.6
  120.1 0.0 copy-done
  120.1 0.9 fusion.59
  121.1 0.2 copy-done.6
  121.3 1.2 fusion.6
  122.5 1.2 convolution_convert_fusion.1
  123.7 0.0 copy-start.2
  123.7 1.2 convolution_convert_fusion.2
  124.8 0.0 copy-done.2
  124.8 0.8 fusion.28
  125.6 0.8 fusion.30
  126.4 0.0 copy-start.3
  126.4 1.1 fusion.10
  127.5 0.0 copy-done.3
  127.5 0.7 fusion.56
  128.3 1.5 fusion.12
  129.8 1.1 fusion.11
  130.9 0.1 fusion.55
  131.0 0.8 fusion.17
  131.8 31.4 %gradient_sum.1 = bf16[8,224,128]{2,1,0:T(8,128)(2,1)} custom-call(bf16[8,224,128]{2,1,0:T(8,128)(2,1)} %bitcast.87), custom_call_target="tpu_custom_call" | custom-call | tf_op jit(solution)/shard_map/gradient_sum/pallas_call | solution.py:187
  163.2 1.1 fusion.54
  164.3 0.1 maximum_convert_fusion
  164.4 0.0 copy-start.4
  164.4 0.2 multiply_reduce_fusion.1
  164.7 2.5 %fusion.27 = f32[2048,384]{1,0:T(8,128)} fusion(bf16[2048,192]{0,1:T(8,128)(2,1)S(1)} %convolution_convert_fusion.2, f32[192]{0:T(256)S(1)} %get-tuple-element.31, f32[192]{0:T(256)S(1)} %sqrt.24, f32[576,384]{1,0:T(8,128)S(1)} %maximum_convert_fusion, f32[1,2,192,384]{3,2,1,0:T(8,128)S(1)} %copy-done.2), kind=kOutput, calls=%fused_computation.57 | convolution fusion | flops 302284800 | bytes 4524032 | tf_op jit(solution)/shard_map/dot_general | solution.py:402
  167.2 0.0 copy-done.4
  167.2 4.3 %fusion.3 = bf16[2048,192]{0,1:T(8,128)(2,1)} fusion(bf16[2048,192]{0,1:T(8,128)(2,1)S(1)} %copy-done.4, f32[2048,384]{1,0:T(8,128)} %fusion.27, bf16[2048,192]{0,1:T(8,128)(2,1)S(1)} %convolution_convert_fusion.2, f32[384]{0:T(512)S(1)} %add_rsqrt_fusion.1, f32[384]{0:T(512)S(1)} %sqrt.26, f32[192]{0:T(256)S(1)} %get-tuple-element.30, f32[192]{0:T(256)S(1)} %sqrt.25, ...), kind=kOutput, calls=%fused_computation.11 | convolution fusion | flops 610467840 | bytes 6690816 | tf_op jit(solution)/shard_map/dot_general | solution.py:405
  (13 shorter events, 0.2 us)
Async XLA Ops:
  0.0 120.1 %copy-start = (bf16[768,1]{0,1:T(2,128)(2,1)S(1)}, bf16[768,1]{0,1:T(2,128)(2,1)}, u32[]{:S(2)}) copy-start(bf16[768,1]{0,1:T(2,128)(2,1)} %param.19) | copy-start | bytes 4612
  112.9 2.8 %copy-start.1 = (bf16[4,512,768]{2,1,0:T(8,128)(2,1)S(1)}, bf16[4,512,768]{2,1,0:T(8,128)(2,1)}, u32[]{:S(2)}) copy-start(bf16[4,512,768]{2,1,0:T(8,128)(2,1)} %head_gather.1) | copy-start | bytes 9437188
  112.9 6.4 %copy-start.5 = (f32[768]{0:T(1024)S(1)}, f32[768]{0:T(1024)}, u32[]{:S(2)}) copy-start(f32[768]{0:T(1024)} %param.17) | copy-start | bytes 9220
  120.1 1.2 copy-start.6
  123.7 1.2 copy-start.2
  126.4 1.2 copy-start.3
  164.4 2.8 %copy-start.4 = (bf16[2048,192]{0,1:T(8,128)(2,1)S(1)}, bf16[2048,192]{0,1:T(8,128)(2,1)}, u32[]{:S(2)}) copy-start(bf16[2048,192]{0,1:T(8,128)(2,1)} %copy.15) | copy-start | bytes 2359300

commit v2 on v1

--- a/solution.py
+++ b/solution.py
@@ -127,36 +127,6 @@
     )(x)
 
 
-def gather_kernel(nh, x_ref, o_ref, send, recv):
-    seq, head = lax.axis_index("seq"), lax.axis_index("head")
-    partner, peer = head_pals(nh, head)
-    greet([(seq, partner), (seq, peer)])
-    to_peer = remote(x_ref, o_ref.at[head], send.at[0], recv.at[0], (seq, peer))
-    to_partner = remote(x_ref, o_ref.at[head], send.at[1], recv.at[1], (seq, partner))
-    to_peer.start()
-    to_partner.start()
-    o_ref[head] = x_ref[...]
-    to_peer.wait_recv()
-    forward = remote(o_ref.at[peer], o_ref.at[peer], send.at[2], recv.at[2], (seq, partner))
-    forward.start()
-    to_peer.wait_send()
-    to_partner.wait()
-    forward.wait()
-
-
-def head_gather(x, nh):
-    dma = pltpu.SemaphoreType.DMA
-    return pl.pallas_call(
-        functools.partial(gather_kernel, nh),
-        out_shape=jax.ShapeDtypeStruct((nh,) + x.shape, x.dtype),
-        in_specs=[VMEM],
-        out_specs=VMEM,
-        scratch_shapes=[dma((3,)), dma((3,))],
-        compiler_params=comm_params(3),
-        name="head_gather",
-    )(x)
-
-
 def sum_kernel(n, x_ref, o_ref, held, send, recv, send_b, recv_b):
     seq, head = lax.axis_index("seq"), lax.axis_index("head")
     targets = others(n, seq)
@@ -198,26 +168,105 @@
     )(x)
 
 
-def pick_kernel(index_ref, x_ref, o_ref):
-    o_ref[...] = x_ref[...]
-
-
-def pick_blocks(x, index):
-    block = (1,) + x.shape[1:]
-    return pl.pallas_call(
-        pick_kernel,
-        out_shape=jax.ShapeDtypeStruct(index.shape + x.shape[1:], x.dtype),
-        grid_spec=pltpu.PrefetchScalarGridSpec(
-            num_scalar_prefetch=1,
-            grid=index.shape,
-            in_specs=[pl.BlockSpec(block, lambda i, index: (index[i], 0, 0))],
-            out_specs=pl.BlockSpec(block, lambda i, index: (i, 0, 0)),
+def route_kernel(nh, dest_ref, image_ref, x_ref, o_ref, m_ref, sems):
+    head = lax.axis_index("head")
+    part = o_ref.shape[1]
+    pairs = dest_ref.shape[0] // 2
+    m_ref[...] = jnp.full(m_ref.shape, -1, jnp.int32)
+
+    def piece(pair):
+        dest = dest_ref[2 * pair]
+        known = jnp.maximum(dest, 0)
+        offset = head * part
+        slot = 2 * pair + lax.rem(known + lax.div(offset, BLK), 2)
+        start = pl.multiple_of(slot * BLK + lax.rem(offset, BLK), part)
+        target = lax.div(known, BLK_DEV)
+        copy = pltpu.make_async_copy(x_ref.at[pl.ds(start, part)], o_ref.at[target], sems.at[pair])
+        return dest, target, copy
+
+    for pair in range(pairs):
+        dest, target, copy = piece(pair)
+
+        @pl.when(dest >= 0)
+        def _():
+            copy.start()
+            same = (image_ref[2 * pair] == image_ref[2 * pair + 1]).astype(jnp.int32)
+            code = 2 * lax.div(lax.rem(dest, BLK_DEV), 2) + same
+            m_ref[target] = jnp.full(m_ref.shape[1:], code, jnp.int32)
+
+    for pair in range(pairs):
+        dest, target, copy = piece(pair)
+
+        @pl.when(dest >= 0)
+        def _():
+            copy.wait()
+
+
+def route(slot_dest, slot_image, patches, n, nh):
+    smem = pl.BlockSpec(memory_space=pltpu.SMEM)
+    part = PAIR // nh
+    return pl.pallas_call(
+        functools.partial(route_kernel, nh),
+        out_shape=(
+            jax.ShapeDtypeStruct((n, part, patches.shape[1]), patches.dtype),
+            jax.ShapeDtypeStruct((n, 8, LANES), jnp.int32),
         ),
-        name="pick_blocks",
-    )(index, x)
-
-
-def encode_kernel(flag_ref, x_ref, w_ref, gain_ref, o_ref, q_ref, k_ref, v_ref, a_ref):
+        in_specs=[smem, smem, pl.BlockSpec(memory_space=pl.ANY)],
+        out_specs=(VMEM, VMEM),
+        scratch_shapes=[pltpu.SemaphoreType.DMA((slot_dest.shape[0] // 2,))],
+        compiler_params=pltpu.CompilerParams(vmem_limit_bytes=56 * 1024 * 1024),
+        name="route_pairs",
+    )(slot_dest, slot_image, patches)
+
+
+def select_kernel(code_ref, x_ref, o_ref, same_ref, sems):
+    head = lax.axis_index("head")
+    same_ref[0] = 0
+
+    def begin(source, carry):
+        code = code_ref[source]
+
+        @pl.when(code >= 0)
+        def _():
+            pair = lax.div(code, 2)
+            pltpu.make_async_copy(x_ref.at[source], o_ref.at[pair], sems.at[pair]).start()
+
+            @pl.when(pair == head)
+            def _():
+                same_ref[0] = lax.rem(code, 2)
+
+        return carry
+
+    lax.fori_loop(0, code_ref.shape[0], begin, 0)
+    for pair in range(o_ref.shape[0]):
+        pltpu.make_async_copy(x_ref.at[0], o_ref.at[pair], sems.at[pair]).wait()
+
+
+def select(codes, arrived, pairs):
+    smem = pl.BlockSpec(memory_space=pltpu.SMEM)
+    return pl.pallas_call(
+        select_kernel,
+        out_shape=(
+            jax.ShapeDtypeStruct((pairs,) + arrived.shape[1:], arrived.dtype),
+            jax.ShapeDtypeStruct((1,), jnp.int32),
+        ),
+        in_specs=[smem, pl.BlockSpec(memory_space=pl.ANY)],
+        out_specs=(VMEM, smem),
+        scratch_shapes=[pltpu.SemaphoreType.DMA((pairs,))],
+        compiler_params=pltpu.CompilerParams(vmem_limit_bytes=24 * 1024 * 1024),
+        name="select_pairs",
+    )(codes, arrived)
+
+
+CHUNK = 128
+
+
+def encode_kernel(
+    nh, flag_ref, x_ref, w_ref, gain_ref, o_ref, q_ref, k_ref, v_ref, a_ref, send, recv
+):
+    seq, head = lax.axis_index("seq"), lax.axis_index("head")
+    partner, peer = head_pals(nh, head)
+    greet([(seq, partner), (seq, peer)])
     width = x_ref.shape[1]
     wide = x_ref[...].astype(jnp.float32)
     factor = lax.rsqrt(jnp.mean(wide * wide, axis=-1, keepdims=True) + EPSILON)
@@ -233,45 +282,73 @@
     v_ref[...] = project(2)
     apart = jnp.where(flag_ref[0] > 0, 0.0, -1e30).astype(jnp.float32)
     key_block = lax.broadcasted_iota(jnp.int32, (1, PAIR), 1) // BLK
-    first = lax.broadcasted_iota(jnp.int32, (BLK, LANES), 1) < HDIM
-
-    def slab(index, carry):
-        columns = pl.ds(pl.multiple_of(index * LANES, LANES), LANES)
-        keys = k_ref[:, columns]
-        values = v_ref[:, columns]
-        for block in range(2):
-            rows = pl.ds(block * BLK, BLK)
-            bias = jnp.where(key_block == block, 0.0, apart)
-            query = q_ref[rows, columns]
-            halves = []
-            for half in range(2):
-                chosen = first if half == 0 else jnp.logical_not(first)
-                own = jnp.where(chosen, query, jnp.zeros_like(query))
-                scores = lax.dot_general(own, keys, NT, preferred_element_type=jnp.float32) + bias
+    first = lax.broadcasted_iota(jnp.int32, (CHUNK, LANES), 1) < HDIM
+    direct = []
+    forwards = []
+
+    for chunk in range(PAIR // CHUNK):
+        rows = pl.ds(chunk * CHUNK, CHUNK)
+        bias = jnp.where(key_block == chunk * CHUNK // BLK, 0.0, apart)
+
+        def slabs(index, carry):
+            for inner in range(2):
+                columns = pl.ds(pl.multiple_of((2 * index + inner) * LANES, LANES), LANES)
+                query = q_ref[rows, columns]
+                nothing = jnp.zeros_like(query)
+                both = jnp.concatenate(
+                    [jnp.where(first, query, nothing), jnp.where(first, nothing, query)], axis=0
+                )
+                scores = lax.dot_general(
+                    both, k_ref[:, columns], NT, preferred_element_type=jnp.float32
+                ) + bias
                 top = jnp.max(scores, axis=-1, keepdims=True)
                 weights = jnp.exp(scores - top)
                 total = jnp.sum(weights, axis=-1, keepdims=True)
                 mixed = jnp.dot(
-                    weights.astype(jnp.bfloat16), values, preferred_element_type=jnp.float32
+                    weights.astype(jnp.bfloat16),
+                    v_ref[:, columns],
+                    preferred_element_type=jnp.float32,
+                ) * (1.0 / total)
+                a_ref[:, columns] = jnp.where(first, mixed[:CHUNK], mixed[CHUNK:]).astype(
+                    jnp.bfloat16
                 )
-                halves.append(mixed * (1.0 / total))
-            a_ref[rows, columns] = jnp.where(first, halves[0], halves[1]).astype(jnp.bfloat16)
-        return carry
-
-    lax.fori_loop(0, width // LANES, slab, 0)
-    mixed = jnp.dot(a_ref[...], w_ref[3].reshape(width, width), preferred_element_type=jnp.float32)
-    o_ref[...] = (x_ref[...].astype(jnp.float32) + mixed).astype(jnp.bfloat16)
-
-
-def encode(flag, rows, weights, gain):
-    return pl.pallas_call(
-        encode_kernel,
-        out_shape=jax.ShapeDtypeStruct(rows.shape, rows.dtype),
+            return carry
+
+        lax.fori_loop(0, width // LANES // 2, slabs, 0)
+        mixed = jnp.dot(
+            a_ref[...], w_ref[3].reshape(width, width), preferred_element_type=jnp.float32
+        )
+        o_ref[head, rows] = (x_ref[rows].astype(jnp.float32) + mixed).astype(jnp.bfloat16)
+        mine = o_ref.at[head, rows]
+        to_peer = remote(mine, mine, send.at[0, chunk], recv.at[0, chunk], (seq, peer))
+        to_partner = remote(mine, mine, send.at[1, chunk], recv.at[1, chunk], (seq, partner))
+        to_peer.start()
+        to_partner.start()
+        direct.append((to_peer, to_partner))
+    for chunk, (to_peer, to_partner) in enumerate(direct):
+        to_peer.wait_recv()
+        theirs = o_ref.at[peer, pl.ds(chunk * CHUNK, CHUNK)]
+        forward = remote(theirs, theirs, send.at[2, chunk], recv.at[2, chunk], (seq, partner))
+        forward.start()
+        forwards.append(forward)
+    for (to_peer, to_partner), forward in zip(direct, forwards):
+        to_peer.wait_send()
+        to_partner.wait()
+        forward.wait()
+
+
+def encode_and_gather(flag, rows, weights, gain, nh):
+    dma = pltpu.SemaphoreType.DMA
+    chunks = PAIR // CHUNK
+    return pl.pallas_call(
+        functools.partial(encode_kernel, nh),
+        out_shape=jax.ShapeDtypeStruct((nh,) + rows.shape, rows.dtype),
         in_specs=[pl.BlockSpec(memory_space=pltpu.SMEM), VMEM, VMEM, VMEM],
         out_specs=VMEM,
-        scratch_shapes=[pltpu.VMEM(rows.shape, jnp.bfloat16)] * 4,
-        compiler_params=pltpu.CompilerParams(vmem_limit_bytes=56 * 1024 * 1024),
-        name="encode_pair",
+        scratch_shapes=[pltpu.VMEM(rows.shape, jnp.bfloat16)] * 3
+        + [pltpu.VMEM((CHUNK, rows.shape[1]), jnp.bfloat16), dma((3, chunks)), dma((3, chunks))],
+        compiler_params=comm_params(3),
+        name="encode_and_gather",
     )(flag, rows, weights, gain)
 
 
@@ -324,35 +401,13 @@
     head = lax.axis_index("head")
     width = w_out.shape[0]
     model = patches.shape[1]
-    part = PAIR // nh
-    shard_pairs = BLK_DEV // 2
-
-    first_dest = slot_dest[0::2]
-    same_image = (slot_image[0::2] == slot_image[1::2]).astype(jnp.int32)
-    pair_dest = first_dest // 2
-    goes = (pair_dest[None, :] // shard_pairs == jnp.arange(n)[:, None]) & (first_dest >= 0)[None, :]
-    has = jnp.any(goes, axis=1)
-    offset = head * part
-    slot = 2 * jnp.arange(first_dest.shape[0]) + (first_dest + offset // BLK) % 2
-    start = (slot * BLK + offset % BLK) // part
-    send_index = jnp.sum(jnp.where(goes, start[None, :], 0), axis=1).astype(jnp.int32)
-    code = jnp.sum(
-        jnp.where(goes, (2 * (pair_dest % shard_pairs) + same_image)[None, :], 0), axis=1
-    )
-    code = jnp.where(has, code, -1).astype(jnp.int32)
-    meta = jnp.broadcast_to(code[:, None, None], (n, 8, LANES))
-    sending = pick_blocks(patches.reshape(-1, part, model), send_index)
+    sending, meta = route(slot_dest, slot_image, patches, n, nh)
     weights = jnp.concatenate([jnp.swapaxes(w_qkv, 1, 2), w_out[None]], axis=0)
     arrived, codes, full_weights = enter(sending, meta, weights, n, nh)
-    codes = codes[:, 0, 0]
-    source = (codes[None, :] >= 0) & (codes[None, :] // 2 == jnp.arange(shard_pairs)[:, None])
-    source_index = jnp.sum(jnp.where(source, jnp.arange(n)[None, :], 0), axis=1).astype(jnp.int32)
-    same = jnp.sum(
-        jnp.where((codes >= 0) & (codes // 2 == head), codes % 2, 0)
-    ).astype(jnp.int32)
-    own_pair = head_swap(pick_blocks(arrived, source_index), nh).reshape(PAIR, model)
-    own_embedded = encode(same.reshape(1), own_pair, full_weights, enc_gain[None, :])
-    full_embedded = head_gather(own_embedded, nh).reshape(nh * PAIR, model)
+    chosen, same = select(codes[:, 0, 0], arrived, BLK_DEV // 2)
+    own_pair = head_swap(chosen, nh).reshape(PAIR, model)
+    full_embedded = encode_and_gather(same, own_pair, full_weights, enc_gain[None, :], nh)
+    full_embedded = full_embedded.reshape(nh * PAIR, model)
     embedded = lax.dynamic_slice_in_dim(full_embedded, head * width, width, 1)
 
     normed_fast = norm_rows(full_embedded, fast_gain)

time: 172 us -> 156 us (0.907)
  Pallas kernels: 134 us -> 121 us
  other arithmetic: 9.39 us -> 7.2 us
    pallas_call x4 -> x3, Pallas kernels: 49.8 us -> 36.5 us  [the longest x1 31.1 us: encode_and_gather(): pl.pallas_call(functools.partial(encode_kernel, nh), out_shape=jax.ShapeD...]
    unnamed x15 -> x19, local copies, waits for them, and re-layouts: 2.49 us -> 4.77 us
    slice x4 -> x1, local copies, waits for them, and re-layouts: 3.24 us -> 0.99 us  [on_device(): chosen, same = select(codes[:, 0, 0], arrived, BLK_DEV // 2)]
    reduce_sum x3 -> x0, other arithmetic: 2.02 us -> none  [the longest x1 0.71 us: on_device(): jnp.sum(jnp.where(goes, (2 * (pair_dest % shard_pairs) + same_image)[None...]
where the time goes in v2:
time: 156 us; the launch traced here: 155 us
  Pallas kernels  121 us (78%)
  matrix products  17.2 us (11%)
  local copies, waits for them, and re-layouts  9.67 us (6%)
  other arithmetic  7.2 us (5%)
    pallas_call x1, Pallas kernels, enter(): pl.pallas_call(functools.partial(entry_kernel, n, nh), out_shape=(jax.Sha...  40.2 us
    pallas_call x1, Pallas kernels, seq_sum(): pl.pallas_call(functools.partial(sum_kernel, n), out_shape=jax.ShapeDtype...  31.4 us
    pallas_call x1, Pallas kernels, encode_and_gather(): pl.pallas_call(functools.partial(encode_kernel, nh), out_shape=jax.ShapeD...  31.1 us
    pallas_call x1, Pallas kernels, head_swap(): pl.pallas_call(functools.partial(swap_kernel, nh), out_shape=jax.ShapeDty...  12.6 us
    unnamed x19, local copies, waits for them, and re-layouts  4.77 us
    dot_general x1, matrix products, on_device(): jnp.dot(query_hidden, applied_down.T, preferred_element_type=jnp.float32)  4.34 us
    pallas_call x1, Pallas kernels, route(): pl.pallas_call(functools.partial(route_kernel, nh), out_shape=(jax.ShapeD...  3.19 us

profile of v2, /device:TPU:24, one launch (start us, length us, event | category | flops | bytes accessed | tf_op | source)
XLA Modules:
  0.0 155.0 jit_solution(11574950341660618876)
XLA Ops:
  0.0 0.0 copy-start
  0.0 1.3 broadcast_in_dim.5.gain_ref
  1.3 2.5 %pad_maximum_fusion.w_ref = bf16[4,192,768]{2,1,0:T(8,128)(2,1)} fusion(bf16[1,192,768]{2,1,0:T(8,128)(2,1)} %bitcast.87, bf16[3,192,768]{2,1,0:T(8,128)(2,1)} %bitcast.86), kind=kLoop, calls=%fused_computation.21 | loop fusion | flops 589824 | bytes 2359296 | tf_op jit(solution)/shard_map/concatenate | solution.py:405
  3.8 3.2 %route_pairs.1 = (bf16[8,128,768]{2,1,0:T(8,128)(2,1)}, s32[8,8,128]{2,1,0:T(8,128)}) custom-call(s32[16]{0:T(128)} %dest_ref.1, s32[16]{0:T(128)} %image_ref.1, bf16[4096,768]{1,0:T(8,128)(2,1)} %x_ref.1), custom_call_target="tpu_custom_call" | custom-call | tf_op jit(solution)/shard_map/route_pairs/pallas_call | solution.py:208
  7.0 40.2 %entry_exchange.1 = (bf16[8,128,768]{2,1,0:T(8,128)(2,1)}, s32[8,8,128]{2,1,0:T(8,128)}, bf16[4,4,192,768]{3,2,1,0:T(8,128)(2,1)}) custom-call(bf16[8,128,768]{2,1,0:T(8,128)(2,1)} %get-tuple-element.12.x_ref, s32[8,8,128]{2,1,0:T(8,128)} %get-tuple-element.13.m_ref, bf16[4,192,768]{2,1,0:T(8,128)(2,1)} %pad_maximum_fusion.w_ref), custom_call_target="tpu_custom_call" | custom-call | tf_op jit(solution)/shard_map/entry_exchange/pallas_call | solution.py:83
  47.2 1.0 slice_reduce_fusion.code_ref
  48.2 0.0 copy-start.1
  48.2 1.4 copy-done.1
  49.6 2.2 %select_pairs.1 = (bf16[4,128,768]{2,1,0:T(8,128)(2,1)S(1)}, s32[1]{0:T(128)}) custom-call(s32[8]{0:T(128)S(1)} %slice_reduce_fusion.code_ref, bf16[8,128,768]{2,1,0:T(8,128)(2,1)S(1)} %copy-done.1), custom_call_target="tpu_custom_call" | custom-call | tf_op jit(solution)/shard_map/select_pairs/pallas_call | solution.py:247
  51.8 0.0 copy-start.2
  51.9 0.9 copy-done.2
  52.7 12.6 %head_swap.1 = bf16[4,128,768]{2,1,0:T(8,128)(2,1)} custom-call(bf16[4,128,768]{2,1,0:T(8,128)(2,1)} %copy-done.2), custom_call_target="tpu_custom_call" | custom-call | tf_op jit(solution)/shard_map/head_swap/pallas_call | solution.py:119
  65.3 31.1 %encode_and_gather.1 = bf16[4,512,768]{2,1,0:T(8,128)(2,1)} custom-call(s32[1]{0:T(128)} %get-tuple-element.16.flag_ref, bf16[512,768]{1,0:T(8,128)(2,1)} %bitcast.83, bf16[4,4,192,768]{3,2,1,0:T(8,128)(2,1)} %get-tuple-element.18.w_ref, f32[1,768]{1,0:T(1,128)} %broadcast_in_dim.5.gain_ref), custom_call_target="tpu_custom_call" | custom-call | tf_op jit(solution)/shard_map/encode_and_gather/pallas_call | solution.py:343
  96.4 0.0 copy-start.3
  96.4 0.0 copy-start.7
  96.4 2.7 %fusion = f32[4,512]{1,0:T(4,128)S(1)} fusion(bf16[4,512,768]{2,1,0:T(8,128)(2,1)} %encode_and_gather.1), kind=kLoop, calls=%fused_computation.2 | loop fusion | flops 4716544 | bytes 3153920 | tf_op jit(solution)/shard_map/reduce_sum | solution.py:357
  99.2 0.1 copy-done.3
  99.2 1.4 constant_dynamic-slice_fusion
  100.7 2.2 %copy.14 = bf16[2048,192]{0,1:T(8,128)(2,1)} copy(bf16[2048,192]{1,0:T(8,128)(2,1)} %constant_dynamic-slice_fusion) | data formatting | bytes 1572864
  102.9 0.0 copy-done.7
  102.9 0.8 fusion.2
  103.7 0.0 copy-start.8
  103.7 0.0 copy-done
  103.7 0.9 fusion.51
  104.6 0.2 copy-done.8
  104.8 1.2 fusion.6
  106.0 1.2 convolution_convert_fusion.1
  107.2 0.0 copy-start.4
  107.2 1.2 convolution_convert_fusion.2
  108.4 0.0 copy-done.4
  108.4 0.8 fusion.28
  109.1 0.8 fusion.30
  109.9 0.0 copy-start.5
  109.9 1.1 fusion.10
  111.1 0.0 copy-done.5
  111.1 0.7 fusion.48
  111.8 1.5 fusion.12
  113.3 1.1 fusion.11
  114.4 0.1 fusion.47
  114.5 0.8 fusion.17
  115.3 31.4 %gradient_sum.1 = bf16[8,224,128]{2,1,0:T(8,128)(2,1)} custom-call(bf16[8,224,128]{2,1,0:T(8,128)(2,1)} %bitcast.84), custom_call_target="tpu_custom_call" | custom-call | tf_op jit(solution)/shard_map/gradient_sum/pallas_call | solution.py:157
  146.8 1.1 fusion.46
  147.8 0.1 maximum_convert_fusion
  147.9 0.0 copy-start.6
  147.9 0.2 multiply_reduce_fusion.1
  148.2 2.5 %fusion.27 = f32[2048,384]{1,0:T(8,128)} fusion(bf16[2048,192]{0,1:T(8,128)(2,1)S(1)} %convolution_convert_fusion.2, f32[192]{0:T(256)S(1)} %get-tuple-element.32, f32[192]{0:T(256)S(1)} %sqrt.24, f32[576,384]{1,0:T(8,128)S(1)} %maximum_convert_fusion, f32[1,2,192,384]{3,2,1,0:T(8,128)S(1)} %copy-done.4), kind=kOutput, calls=%fused_computation.57 | convolution fusion | flops 302284800 | bytes 4524032 | tf_op jit(solution)/shard_map/dot_general | solution.py:457
  150.7 0.0 copy-done.6
  150.7 4.3 %fusion.3 = bf16[2048,192]{0,1:T(8,128)(2,1)} fusion(bf16[2048,192]{0,1:T(8,128)(2,1)S(1)} %copy-done.6, f32[2048,384]{1,0:T(8,128)} %fusion.27, bf16[2048,192]{0,1:T(8,128)(2,1)S(1)} %convolution_convert_fusion.2, f32[384]{0:T(512)S(1)} %add_rsqrt_fusion.1, f32[384]{0:T(512)S(1)} %sqrt.26, f32[192]{0:T(256)S(1)} %get-tuple-element.31, f32[192]{0:T(256)S(1)} %sqrt.25, ...), kind=kOutput, calls=%fused_computation.11 | convolution fusion | flops 610467840 | bytes 6690816 | tf_op jit(solution)/shard_map/dot_general | solution.py:460
  (8 shorter events, 0.1 us)
Async XLA Ops:
  0.0 103.7 %copy-start = (bf16[768,1]{0,1:T(2,128)(2,1)S(1)}, bf16[768,1]{0,1:T(2,128)(2,1)}, u32[]{:S(2)}) copy-start(bf16[768,1]{0,1:T(2,128)(2,1)} %param.19) | copy-start | bytes 4612
  48.2 1.4 copy-start.1
  51.8 0.9 copy-start.2
  96.4 2.8 %copy-start.3 = (bf16[4,512,768]{2,1,0:T(8,128)(2,1)S(1)}, bf16[4,512,768]{2,1,0:T(8,128)(2,1)}, u32[]{:S(2)}) copy-start(bf16[4,512,768]{2,1,0:T(8,128)(2,1)} %encode_and_gather.1) | copy-start | bytes 9437188
  96.4 6.4 %copy-start.7 = (f32[768]{0:T(1024)S(1)}, f32[768]{0:T(1024)}, u32[]{:S(2)}) copy-start(f32[768]{0:T(1024)} %param.17) | copy-start | bytes 9220
  103.7 1.2 copy-start.8
  107.2 1.2 copy-start.4
  109.9 1.2 copy-start.5
  147.9 2.8 %copy-start.6 = (bf16[2048,192]{0,1:T(8,128)(2,1)S(1)}, bf16[2048,192]{0,1:T(8,128)(2,1)}, u32[]{:S(2)}) copy-start(bf16[2048,192]{0,1:T(8,128)(2,1)} %copy.14) | copy-start | bytes 2359300
